TPU v7x, 16 devices: a whole 2x2x2 slice. The times are simulated.
16 devices in a mesh: fsdp: 16 (over z, y, x, core).
Axes of the slice: x: 2, y: 2, z: 2, core: 2. Of those that a mesh axis runs over, the one named last changes fastest.
Arguments:
- x_saved: bfloat16 [2, 2, 16, 2048, 512], P(None, None, 'fsdp')
- grad_out: bfloat16 [2, 16, 2048, 512], P(None, 'fsdp')
- x_next: bfloat16 [2, 16, 2048, 512], P(None, 'fsdp')
- w_up: bfloat16 [2, 2, 512, 2048], replicated
- w_down: bfloat16 [2, 2, 2048, 512], replicated
- acc_up: float32 [2, 2, 512, 2048], P(None, None, 'fsdp')
- acc_down: float32 [2, 2, 2048, 512], P(None, None, 'fsdp')
- master_up: float32 [2, 2, 512, 2048], P(None, None, 'fsdp')
- master_down: float32 [2, 2, 2048, 512], P(None, None, 'fsdp')
- moment1_up: float32 [2, 2, 512, 2048], P(None, None, 'fsdp')
- moment1_down: float32 [2, 2, 2048, 512], P(None, None, 'fsdp')
- moment2_up: float32 [2, 2, 512, 2048], P(None, None, 'fsdp')
- moment2_down: float32 [2, 2, 2048, 512], P(None, None, 'fsdp')
Outputs:
- output 1: float32 [2, 2, 512, 2048], P(None, None, 'fsdp')
- output 2: float32 [2, 2, 2048, 512], P(None, None, 'fsdp')
- output 3: float32 [2, 2, 512, 2048], P(None, None, 'fsdp')
- output 4: float32 [2, 2, 2048, 512], P(None, None, 'fsdp')
- output 5: float32 [2, 2, 512, 2048], P(None, None, 'fsdp')
- output 6: float32 [2, 2, 2048, 512], P(None, None, 'fsdp')
- output 7: bfloat16 [2, 16, 2048, 512], P(None, 'fsdp')
All inputs are finite; a program needn't handle non-finite values.
Results may differ from a plain program's by a relative error of at most 0.00799662.
Values are sent between devices in bfloat16 or wider.
A program may use at most 1 GiB of HBM per device.

v0:
```python
import jax
import jax.numpy as jnp
from jax import lax
from jax.sharding import PartitionSpec as P

LEARN_RATE = 0.005
BETA_ONE = 0.9
BETA_TWO = 0.95
ADAM_EPS = 1e-8
WEIGHT_DECAY = 0.1
MICROBATCHES = 2
ADAM_STEP = 2


def adam_update(acc_part, grad_new, master, moment_one, moment_two):
    grad_mean = (acc_part + grad_new) / MICROBATCHES
    moment_one = BETA_ONE * moment_one + (1.0 - BETA_ONE) * grad_mean
    moment_two = BETA_TWO * moment_two + (1.0 - BETA_TWO) * grad_mean * grad_mean
    corr_one = 1.0 - BETA_ONE ** ADAM_STEP
    corr_two = 1.0 - BETA_TWO ** ADAM_STEP
    step_dir = (moment_one / corr_one) / (jnp.sqrt(moment_two / corr_two) + ADAM_EPS)
    master = master - LEARN_RATE * (step_dir + WEIGHT_DECAY * master)
    return master, moment_one, moment_two


def backward_layer(x_in, cotangent, w_one, w_two):
    hidden = jnp.einsum('bsd,df->bsf', x_in, w_one, preferred_element_type=jnp.float32)
    gelu_out, gelu_vjp = jax.vjp(jax.nn.gelu, hidden)
    grad_act = jnp.einsum('bsd,fd->bsf', cotangent, w_two, preferred_element_type=jnp.float32)
    grad_hidden = gelu_vjp(grad_act)[0].astype(jnp.bfloat16)
    part_down = jnp.einsum('bsf,bsd->fd', gelu_out.astype(jnp.bfloat16), cotangent, preferred_element_type=jnp.float32)
    part_up = jnp.einsum('bsd,bsf->df', x_in, grad_hidden, preferred_element_type=jnp.float32)
    return part_up, part_down, grad_hidden


def forward_layer(x_in, w_one, w_two):
    hidden = jnp.einsum('bsd,df->bsf', x_in, w_one, preferred_element_type=jnp.float32)
    gelu_out = jax.nn.gelu(hidden).astype(jnp.bfloat16)
    mlp_val = jnp.einsum('bsf,fd->bsd', gelu_out, w_two, preferred_element_type=jnp.float32)
    return (x_in.astype(jnp.float32) + mlp_val).astype(jnp.bfloat16)


def scatter_sum(part, groups):
    received = lax.all_to_all(part.astype(jnp.bfloat16), 'fsdp', 0, 0, tiled=True)
    return jnp.sum(received.reshape((groups, -1) + received.shape[1:]), axis=0, dtype=jnp.float32)


def solution(mesh):
    groups = mesh.shape['fsdp']
    tok_spec = P(None, 'fsdp')
    layer_spec = P(None, None, 'fsdp')
    rep_spec = P()

    def device_step(x_saved, grad_out, x_next, w_up, w_down, acc_up, acc_down, master_up, master_down, moment1_up, moment1_down, moment2_up, moment2_down):
        stages = x_saved.shape[0]
        layers = x_saved.shape[1]
        state_lists = [[], [], [], [], [], []]
        y_list = []
        for stage_id in range(stages):
            cotangent = grad_out[stage_id]
            stage_state = [[None] * layers for state_id in range(6)]
            full_up = [None] * layers
            full_down = [None] * layers
            for layer_id in reversed(range(layers)):
                cur_up = w_up[stage_id, layer_id]
                cur_down = w_down[stage_id, layer_id]
                part_up, part_down, grad_hidden = backward_layer(x_saved[stage_id, layer_id], cotangent, cur_up, cur_down)
                if layer_id > 0:
                    cotangent = (cotangent.astype(jnp.float32) + jnp.einsum('bsf,df->bsd', grad_hidden, cur_up, preferred_element_type=jnp.float32)).astype(jnp.bfloat16)
                sum_up = scatter_sum(part_up, groups)
                sum_down = scatter_sum(part_down, groups)
                new_up = adam_update(acc_up[stage_id, layer_id], sum_up, master_up[stage_id, layer_id], moment1_up[stage_id, layer_id], moment2_up[stage_id, layer_id])
                new_down = adam_update(acc_down[stage_id, layer_id], sum_down, master_down[stage_id, layer_id], moment1_down[stage_id, layer_id], moment2_down[stage_id, layer_id])
                for state_id in range(3):
                    stage_state[2 * state_id][layer_id] = new_up[state_id]
                    stage_state[2 * state_id + 1][layer_id] = new_down[state_id]
                full_up[layer_id] = lax.all_gather(new_up[0].astype(jnp.bfloat16), 'fsdp', axis=0, tiled=True)
                full_down[layer_id] = lax.all_gather(new_down[0].astype(jnp.bfloat16), 'fsdp', axis=0, tiled=True)
            hidden_x = x_next[stage_id]
            for layer_id in range(layers):
                hidden_x = forward_layer(hidden_x, full_up[layer_id], full_down[layer_id])
            y_list.append(hidden_x)
            for state_id in range(6):
                state_lists[state_id].append(jnp.stack(stage_state[state_id]))
        return tuple(jnp.stack(entry) for entry in state_lists) + (jnp.stack(y_list),)

    return jax.shard_map(device_step, mesh=mesh, in_specs=(layer_spec, tok_spec, tok_spec, rep_spec, rep_spec) + (layer_spec,) * 8, out_specs=(layer_spec,) * 6 + (tok_spec,), check_vma=False)
```

profile of v0, /device:TPU:0, one launch (start us, length us, event | category | flops | bytes accessed | tf_op | source)
XLA Modules:
  0.0 580.0 jit_solution(17096885867790958015)
XLA Ops:
  7.2 12.6 %fusion.125 = f32[2048,2048]{1,0:T(8,128)} fusion(bf16[2,2,512,2048]{3,2,1,0:T(8,128)(2,1)} %param.16, bf16[2,2,1,2048,512]{4,3,2,1,0:T(8,128)(2,1)} %param.13), kind=kOutput, calls=%fused_computation.134 | convolution fusion | flops 4294967296 | bytes 20971520 | tf_op jit(solution)/shard_map/bsd,df->bsf/dot_general | solution.py:27
  19.8 16.0 %fusion.6 = bf16[2048,2048]{1,0:T(8,128)(2,1)S(1)} fusion(f32[2048,2048]{1,0:T(8,128)} %fusion.125, bf16[2,2,2048,512]{3,2,1,0:T(8,128)(2,1)} %param.17, bf16[2,1,2048,512]{3,2,1,0:T(8,128)(2,1)S(1)} %copy-done.26), kind=kOutput, calls=%fused_computation.18 | convolution fusion | flops 4378853376 | bytes 29360128 | tf_op jit(solution)/shard_map/bsd,fd->bsf/dot_general | solution.py:29
  50.3 12.7 %fusion.118 = f32[2048,2048]{1,0:T(8,128)} fusion(bf16[2,2,512,2048]{3,2,1,0:T(8,128)(2,1)} %param.16, bf16[2,2,1,2048,512]{4,3,2,1,0:T(8,128)(2,1)} %param.13), kind=kOutput, calls=%fused_computation.128 | convolution fusion | flops 4294967296 | bytes 20971520 | tf_op jit(solution)/shard_map/bsd,df->bsf/dot_general | solution.py:27
  70.3 12.5 %fusion.111 = f32[2048,2048]{1,0:T(8,128)} fusion(bf16[2,2,512,2048]{3,2,1,0:T(8,128)(2,1)} %param.16, bf16[2,2,1,2048,512]{4,3,2,1,0:T(8,128)(2,1)} %param.13), kind=kOutput, calls=%fused_computation.121 | convolution fusion | flops 4294967296 | bytes 20971520 | tf_op jit(solution)/shard_map/bsd,df->bsf/dot_general | solution.py:27
  82.9 17.6 %fusion.20 = bf16[2048,2048]{1,0:T(8,128)(2,1)} fusion(f32[2048,2048]{1,0:T(8,128)} %fusion.111, bf16[2,2,2048,512]{3,2,1,0:T(8,128)(2,1)} %param.17, bf16[2,1,2048,512]{3,2,1,0:T(8,128)(2,1)S(1)} %copy-done.27), kind=kOutput, calls=%fused_computation.32 | convolution fusion | flops 4378853376 | bytes 29360128 | tf_op jit(solution)/shard_map/bsd,fd->bsf/dot_general | solution.py:29
  100.5 22.1 %fusion.84 = bf16[2048,512]{0,1:T(8,128)(2,1)} fusion(f32[2048,2048]{1,0:T(8,128)} %fusion.118, bf16[2048,512]{1,0:T(8,128)(2,1)} %add_convert_fusion.5, bf16[2,2,2048,512]{3,2,1,0:T(8,128)(2,1)} %param.17, bf16[2,2,1,2048,512]{4,3,2,1,0:T(8,128)(2,1)} %param.13), kind=kOutput, calls=%fused_computation.103 | convolution fusion | flops 8674869248 | bytes 25165824 | tf_op jit(solution)/shard_map/bsd,bsf->df/dot_general | solution.py:32
  122.5 12.7 %fusion.104 = f32[2048,2048]{1,0:T(8,128)} fusion(bf16[2,2,512,2048]{3,2,1,0:T(8,128)(2,1)} %param.16, bf16[2,2,1,2048,512]{4,3,2,1,0:T(8,128)(2,1)} %param.13), kind=kOutput, calls=%fused_computation.115 | convolution fusion | flops 4294967296 | bytes 20971520 | tf_op jit(solution)/shard_map/bsd,df->bsf/dot_general | solution.py:27
  146.5 21.9 %fusion.87 = bf16[2048,512]{0,1:T(8,128)(2,1)} fusion(f32[2048,2048]{1,0:T(8,128)} %fusion.104, bf16[2048,512]{1,0:T(8,128)(2,1)} %add_convert_fusion.4, bf16[2,2,2048,512]{3,2,1,0:T(8,128)(2,1)} %param.17, bf16[2,2,1,2048,512]{4,3,2,1,0:T(8,128)(2,1)} %param.13), kind=kOutput, calls=%fused_computation.104 | convolution fusion | flops 8674869248 | bytes 25165824 | tf_op jit(solution)/shard_map/bsd,bsf->df/dot_general | solution.py:32
  189.4 16.3 %all-to-all-done.2 = bf16[16,32,2048]{2,1,0:T(8,128)(2,1)S(1)} async-done(((bf16[16,32,2048]{2,1,0:T(8,128)(2,1)}), bf16[16,32,2048]{2,1,0:T(8,128)(2,1)S(1)}, u32[]{:S(2)}, u32[]{:S(2)}) %all-to-all-start.2) | async-done | bytes 2097184 | tf_op jit(solution)/shard_map/all_to_all | solution.py:44
  211.0 11.7 %fusion.93 = bf16[2048,512]{1,0:T(8,128)(2,1)} fusion(bf16[2048,512]{1,0:T(8,128)(2,1)} %add_convert_fusion.5, f32[2048,2048]{1,0:T(8,128)} %fusion.118), kind=kOutput, calls=%fused_computation.108 | convolution fusion | flops 4333764608 | bytes 20971520 | tf_op jit(solution)/shard_map/bsf,bsd->fd/dot_general | solution.py:31
  226.9 11.6 %all-to-all-done.5 = bf16[16,128,512]{2,1,0:T(8,128)(2,1)S(1)} async-done(((bf16[16,128,512]{2,1,0:T(8,128)(2,1)}), bf16[16,128,512]{2,1,0:T(8,128)(2,1)S(1)}, u32[]{:S(2)}, u32[]{:S(2)}) %all-to-all-start.5) | async-done | bytes 2097184 | tf_op jit(solution)/shard_map/all_to_all | solution.py:44
  254.7 20.6 %all-to-all-done.4 = bf16[16,128,512]{2,1,0:T(8,128)(2,1)} async-done(((bf16[16,128,512]{2,1,0:T(8,128)(2,1)}), bf16[16,128,512]{2,1,0:T(8,128)(2,1)}, u32[]{:S(2)}, u32[]{:S(2)}) %all-to-all-start.4) | async-done | bytes 2097184 | tf_op jit(solution)/shard_map/all_to_all | solution.py:44
  281.5 24.6 %all-to-all-done.6 = bf16[16,128,512]{2,1,0:T(8,128)(2,1)} async-done(((bf16[16,128,512]{2,1,0:T(8,128)(2,1)}), bf16[16,128,512]{2,1,0:T(8,128)(2,1)}, u32[]{:S(2)}, u32[]{:S(2)}) %all-to-all-start.6) | async-done | bytes 2097184 | tf_op jit(solution)/shard_map/all_to_all | solution.py:44
  313.6 11.8 %fusion.90 = bf16[2048,512]{1,0:T(8,128)(2,1)} fusion(f32[2048,2048]{1,0:T(8,128)} %fusion.111, bf16[2,1,2048,512]{3,2,1,0:T(8,128)(2,1)} %param.14), kind=kOutput, calls=%fused_computation.105 | convolution fusion | flops 4333764608 | bytes 20971520 | tf_op jit(solution)/shard_map/bsf,bsd->fd/dot_general | solution.py:31
  339.4 21.4 %all-to-all-done.7 = bf16[16,128,512]{2,1,0:T(8,128)(2,1)S(1)} async-done(((bf16[16,128,512]{2,1,0:T(8,128)(2,1)}), bf16[16,128,512]{2,1,0:T(8,128)(2,1)S(1)}, u32[]{:S(2)}, u32[]{:S(2)}) %all-to-all-start.7) | async-done | bytes 2097184 | tf_op jit(solution)/shard_map/all_to_all | solution.py:44
  370.5 25.3 %all-to-all-done.3 = bf16[16,32,2048]{2,1,0:T(8,128)(2,1)S(1)} async-done(((bf16[16,32,2048]{2,1,0:T(8,128)(2,1)}), bf16[16,32,2048]{2,1,0:T(8,128)(2,1)S(1)}, u32[]{:S(2)}, u32[]{:S(2)}) %all-to-all-start.3) | async-done | bytes 2097184 | tf_op jit(solution)/shard_map/all_to_all | solution.py:44
  420.1 13.4 %add_convert_fusion.3 = bf16[2048,512]{1,0:T(8,128)(2,1)} fusion(bf16[2048,512]{1,0:T(8,128)(2,1)} %all-gather.11.cloned.1.call-done, bf16[512,2048]{1,0:T(8,128)(2,1)} %all-gather.9.cloned.1.call-done, bf16[2,1,2048,512]{3,2,1,0:T(8,128)(2,1)} %param.15), kind=kOutput, calls=%fused_computation.90 | convolution fusion | flops 8630829056 | bytes 10485760 | tf_op jit(solution)/shard_map/bsf,fd->bsd/dot_general | solution.py:39
  433.6 12.5 %fusion.94 = bf16[1,1,2048,512]{3,2,1,0:T(8,128)(2,1)S(1)} fusion(bf16[2048,512]{1,0:T(8,128)(2,1)} %all-gather.15.cloned.1.call-done, bf16[2048,512]{1,0:T(8,128)(2,1)} %add_convert_fusion.3, bf16[512,2048]{1,0:T(8,128)(2,1)} %all-gather.13.cloned.1.call-done), kind=kOutput, calls=%fused_computation.111 | convolution fusion | flops 8630829056 | bytes 8388608 | tf_op jit(solution)/shard_map/bsf,fd->bsd/dot_general | solution.py:39
  446.1 17.9 %all-gather.17.cloned.1.call-done = bf16[512,2048]{1,0:T(8,128)(2,1)} async-done(((bf16[32,2048]{1,0:T(8,128)(2,1)}), bf16[512,2048]{1,0:T(8,128)(2,1)}) %all-gather.17.cloned.1.call-update) | async-done | bytes 2097168 | tf_op jit(solution)/shard_map/all_gather | solution.py:77
  464.0 30.4 %all-gather.19.cloned.1.call-done = bf16[2048,512]{1,0:T(8,128)(2,1)} async-done(((bf16[128,512]{1,0:T(8,128)(2,1)}), bf16[2048,512]{1,0:T(8,128)(2,1)}) %all-gather.19.cloned.1.call-update) | async-done | bytes 2097168 | tf_op jit(solution)/shard_map/all_gather | solution.py:78
  494.4 13.8 %add_convert_fusion.1 = bf16[2048,512]{1,0:T(8,128)(2,1)} fusion(bf16[2048,512]{1,0:T(8,128)(2,1)} %all-gather.19.cloned.1.call-done, bf16[512,2048]{1,0:T(8,128)(2,1)} %all-gather.17.cloned.1.call-done, bf16[2,1,2048,512]{3,2,1,0:T(8,128)(2,1)} %param.15), kind=kOutput, calls=%fused_computation.88 | convolution fusion | flops 8630829056 | bytes 10485760 | tf_op jit(solution)/shard_map/bsf,fd->bsd/dot_general | solution.py:39
  508.2 16.8 %all-gather.23.cloned.1.call-done = bf16[2048,512]{1,0:T(8,128)(2,1)} async-done(((bf16[128,512]{1,0:T(8,128)(2,1)}), bf16[2048,512]{1,0:T(8,128)(2,1)}) %all-gather.23.cloned.1.call-update) | async-done | bytes 2097168 | tf_op jit(solution)/shard_map/all_gather | solution.py:78
  525.0 30.6 %all-gather.21.cloned.1.call-done = bf16[512,2048]{1,0:T(8,128)(2,1)} async-done(((bf16[32,2048]{1,0:T(8,128)(2,1)}), bf16[512,2048]{1,0:T(8,128)(2,1)}) %all-gather.21.cloned.1.call-update) | async-done | bytes 2097168 | tf_op jit(solution)/shard_map/all_gather | solution.py:77
  555.5 13.4 %fusion.97 = bf16[1,1,2048,512]{3,2,1,0:T(8,128)(2,1)} fusion(bf16[2048,512]{1,0:T(8,128)(2,1)} %all-gather.23.cloned.1.call-done, bf16[2048,512]{1,0:T(8,128)(2,1)} %add_convert_fusion.1, bf16[512,2048]{1,0:T(8,128)(2,1)} %all-gather.21.cloned.1.call-done), kind=kOutput, calls=%fused_computation.112 | convolution fusion | flops 8630829056 | bytes 8388608 | tf_op jit(solution)/shard_map/bsf,fd->bsd/dot_general | solution.py:39
  (129 shorter events, 145.0 us)
Async XLA Ops:
  44.8 97.8 %all-to-all-start.1 = ((bf16[16,32,2048]{2,1,0:T(8,128)(2,1)}), bf16[16,32,2048]{2,1,0:T(8,128)(2,1)S(1)}, u32[]{:S(2)}, u32[]{:S(2)}) async-start(bf16[16,32,2048]{2,1,0:T(8,128)(2,1)} %bitcast.704), calls=%async_computation.1 | async-start | bytes 4194304 | tf_op jit(solution)/shard_map/all_to_all | solution.py:44
  142.5 25.9 %copy-start = (bf16[16,32,2048]{2,1,0:T(8,128)(2,1)}, bf16[16,32,2048]{2,1,0:T(8,128)(2,1)S(1)}, u32[]{:S(2)}) copy-start(bf16[16,32,2048]{2,1,0:T(8,128)(2,1)S(1)} %all-to-all-done.1) | copy-start | bytes 6291460
  142.5 31.6 %all-to-all-start = ((bf16[16,32,2048]{2,1,0:T(8,128)(2,1)}), bf16[16,32,2048]{2,1,0:T(8,128)(2,1)}, u32[]{:S(2)}, u32[]{:S(2)}) async-start(bf16[16,32,2048]{2,1,0:T(8,128)(2,1)} %bitcast.705), calls=%async_computation | async-start | bytes 4194304 | tf_op jit(solution)/shard_map/all_to_all | solution.py:44
  174.1 31.5 %all-to-all-start.2 = ((bf16[16,32,2048]{2,1,0:T(8,128)(2,1)}), bf16[16,32,2048]{2,1,0:T(8,128)(2,1)S(1)}, u32[]{:S(2)}, u32[]{:S(2)}) async-start(bf16[16,32,2048]{2,1,0:T(8,128)(2,1)} %bitcast.706), calls=%async_computation.2 | async-start | bytes 4194304 | tf_op jit(solution)/shard_map/all_to_all | solution.py:44
  207.0 31.5 %all-to-all-start.5 = ((bf16[16,128,512]{2,1,0:T(8,128)(2,1)}), bf16[16,128,512]{2,1,0:T(8,128)(2,1)S(1)}, u32[]{:S(2)}, u32[]{:S(2)}) async-start(bf16[16,128,512]{2,1,0:T(8,128)(2,1)} %bitcast.700), calls=%async_computation.5 | async-start | bytes 4194304 | tf_op jit(solution)/shard_map/all_to_all | solution.py:44
  210.9 14.6 %copy-start.6 = (f32[2,2,32,2048]{3,2,1,0:T(8,128)S(1)}, f32[2,2,32,2048]{3,2,1,0:T(8,128)}, u32[]{:S(2)}) copy-start(f32[2,2,32,2048]{3,2,1,0:T(8,128)} %param.20) | copy-start | bytes 3145732
  210.9 209.2 %all-gather.9.cloned.1.call-start = ((), (), s32[]{:S(2)}) async-start(), calls=%async_computation.8 | async-start | bytes 2228224 | tf_op jit(solution)/shard_map/all_gather | solution.py:77
  211.0 14.5 %copy-start.8 = (f32[2,2,32,2048]{3,2,1,0:T(8,128)S(1)}, f32[2,2,32,2048]{3,2,1,0:T(8,128)}, u32[]{:S(2)}) copy-start(f32[2,2,32,2048]{3,2,1,0:T(8,128)} %param.18) | copy-start | bytes 3145732
  211.0 14.5 %copy-start.10 = (f32[2,2,32,2048]{3,2,1,0:T(8,128)S(1)}, f32[2,2,32,2048]{3,2,1,0:T(8,128)}, u32[]{:S(2)}) copy-start(f32[2,2,32,2048]{3,2,1,0:T(8,128)} %param.22) | copy-start | bytes 3145732
  211.0 14.5 %copy-start.11 = (f32[2,2,32,2048]{3,2,1,0:T(8,128)S(1)}, f32[2,2,32,2048]{3,2,1,0:T(8,128)}, u32[]{:S(2)}) copy-start(f32[2,2,32,2048]{3,2,1,0:T(8,128)} %param.24) | copy-start | bytes 3145732
  238.5 36.8 %all-to-all-start.4 = ((bf16[16,128,512]{2,1,0:T(8,128)(2,1)}), bf16[16,128,512]{2,1,0:T(8,128)(2,1)}, u32[]{:S(2)}, u32[]{:S(2)}) async-start(bf16[16,128,512]{2,1,0:T(8,128)(2,1)} %bitcast.701), calls=%async_computation.4 | async-start | bytes 4194304 | tf_op jit(solution)/shard_map/all_to_all | solution.py:44
  254.7 53.3 %copy-start.5 = (f32[2,2,128,512]{3,2,1,0:T(8,128)S(1)}, f32[2,2,128,512]{3,2,1,0:T(8,128)}, u32[]{:S(2)}) copy-start(f32[2,2,128,512]{3,2,1,0:T(8,128)} %param.21) | copy-start | bytes 3145732
  275.3 30.8 %all-to-all-start.6 = ((bf16[16,128,512]{2,1,0:T(8,128)(2,1)}), bf16[16,128,512]{2,1,0:T(8,128)(2,1)}, u32[]{:S(2)}, u32[]{:S(2)}) async-start(bf16[16,128,512]{2,1,0:T(8,128)(2,1)} %bitcast.703), calls=%async_computation.6 | async-start | bytes 4194304 | tf_op jit(solution)/shard_map/all_to_all | solution.py:44
  278.5 141.6 %all-gather.11.cloned.1.call-start = ((), (), s32[]{:S(2)}) async-start(), calls=%async_computation.9 | async-start | bytes 2228224 | tf_op jit(solution)/shard_map/all_gather | solution.py:78
  281.5 44.0 %copy-start.13 = (f32[128,512]{1,0:T(8,128)}, f32[128,512]{1,0:T(8,128)S(1)}, u32[]{:S(2)}) copy-start(f32[128,512]{1,0:T(8,128)S(1)} %convert_reduce_fusion.3) | copy-start | bytes 786436
  308.0 17.4 %copy-start.17 = (f32[128,512]{1,0:T(8,128)}, f32[128,512]{1,0:T(8,128)S(1)}, u32[]{:S(2)}) copy-start(f32[128,512]{1,0:T(8,128)S(1)} %convert_reduce_fusion.1) | copy-start | bytes 786436
  311.2 122.4 %all-gather.13.cloned.1.call-start = ((), (), s32[]{:S(2)}) async-start(), calls=%async_computation.10 | async-start | bytes 2228224 | tf_op jit(solution)/shard_map/all_gather | solution.py:77
  311.9 121.7 %all-gather.15.cloned.1.call-start = ((), (), s32[]{:S(2)}) async-start(), calls=%async_computation.11 | async-start | bytes 2228224 | tf_op jit(solution)/shard_map/all_gather | solution.py:78
  312.5 151.5 %all-gather.17.cloned.1.call-start = ((), (), s32[]{:S(2)}) async-start(), calls=%async_computation.12 | async-start | bytes 2228224 | tf_op jit(solution)/shard_map/all_gather | solution.py:77
  313.1 181.4 %all-gather.19.cloned.1.call-start = ((), (), s32[]{:S(2)}) async-start(), calls=%async_computation.13 | async-start | bytes 2228224 | tf_op jit(solution)/shard_map/all_gather | solution.py:78
  325.4 35.4 %all-to-all-start.7 = ((bf16[16,128,512]{2,1,0:T(8,128)(2,1)}), bf16[16,128,512]{2,1,0:T(8,128)(2,1)S(1)}, u32[]{:S(2)}, u32[]{:S(2)}) async-start(bf16[16,128,512]{2,1,0:T(8,128)(2,1)} %bitcast.707), calls=%async_computation.7 | async-start | bytes 4194304 | tf_op jit(solution)/shard_map/all_to_all | solution.py:44
  362.2 33.6 %all-to-all-start.3 = ((bf16[16,32,2048]{2,1,0:T(8,128)(2,1)}), bf16[16,32,2048]{2,1,0:T(8,128)(2,1)S(1)}, u32[]{:S(2)}, u32[]{:S(2)}) async-start(bf16[16,32,2048]{2,1,0:T(8,128)(2,1)} %bitcast.702), calls=%async_computation.3 | async-start | bytes 4194304 | tf_op jit(solution)/shard_map/all_to_all | solution.py:44
  365.6 159.4 %all-gather.23.cloned.1.call-start = ((), (), s32[]{:S(2)}) async-start(), calls=%async_computation.15 | async-start | bytes 2228224 | tf_op jit(solution)/shard_map/all_gather | solution.py:78
  370.3 185.3 %all-gather.21.cloned.1.call-start = ((), (), s32[]{:S(2)}) async-start(), calls=%async_computation.14 | async-start | bytes 2228224 | tf_op jit(solution)/shard_map/all_gather | solution.py:77
  (24 other events, 187.3 us)
Sparse Core Ops, SparseCore 0:
  227.0 46.4 all-gather.8
  311.3 37.9 all-gather.10
  351.6 51.5 all-gather.12
  405.3 28.2 all-gather.14
  435.7 28.2 all-gather.16
  466.1 28.2 all-gather.18
  496.7 28.2 all-gather.22
  527.2 28.2 all-gather.20
where the time goes:
time: 588 us; the launch traced here: 580 us
  matrix products  261 us (44%)
  waiting for transfers between devices  224 us (38%)
  other arithmetic  44 us (7%)
  starting transfers between devices  33.1 us (6%)
  between operations  14.8 us (3%)
    all_to_all x8, waiting for transfers between devices, scatter_sum(): lax.all_to_all(part.astype(jnp.bfloat16), 'fsdp', 0, 0, tiled=True)  126 us
    dot_general x4, matrix products, backward_layer(): jnp.einsum('bsd,bsf->df', x_in, grad_hidden, preferred_element_type=jnp.f...  62.8 us
    dot_general x4, matrix products, forward_layer(): jnp.einsum('bsf,fd->bsd', gelu_out, w_two, preferred_element_type=jnp.flo...  53.1 us
    dot_general x4, matrix products, backward_layer(): jnp.einsum('bsd,df->bsf', x_in, w_one, preferred_element_type=jnp.float32)  50.5 us
    all_gather x4, waiting for transfers between devices, device_step(): lax.all_gather(new_up[0].astype(jnp.bfloat16), 'fsdp', axis=0, tiled=True)  48.5 us
    all_gather x4, waiting for transfers between devices, device_step(): lax.all_gather(new_down[0].astype(jnp.bfloat16), 'fsdp', axis=0, tiled=True)  47.3 us
    dot_general x4, matrix products, backward_layer(): jnp.einsum('bsf,bsd->fd', gelu_out.astype(jnp.bfloat16), cotangent, prefe...  46.2 us
    dot_general x2, matrix products, backward_layer(): jnp.einsum('bsd,fd->bsf', cotangent, w_two, preferred_element_type=jnp.fl...  33.6 us
  transfers between devices with their start and end apart: 16, of which 12 were waited for; matrix products, arithmetic and copies ran while one was open for 43% of the time, Pallas kernels for 0%

commit v1 on v0

v1 whole, which is shorter than its diff:
```python
import jax
import jax.numpy as jnp
from jax import lax
from jax.experimental import pallas as pl
from jax.experimental.pallas import tpu as pltpu
from jax.sharding import PartitionSpec as P

LEARN_RATE = 0.005
BETA_ONE = 0.9
BETA_TWO = 0.95
ADAM_EPS = 1e-8
WEIGHT_DECAY = 0.1
MICROBATCHES = 2
ADAM_STEP = 2
CORR_ONE = 1.0 - BETA_ONE ** ADAM_STEP
CORR_TWO = 1.0 - BETA_TWO ** ADAM_STEP

GELU_A = 0.7978845608028654
GELU_B = 0.044715 * GELU_A

MESH = pl.DeviceIdType.MESH
BF16 = jnp.bfloat16
F32 = jnp.float32

NDEV = 16
SEQ = 2048
D = 512
FF = 2048
FC = 256
NCHUNK = FF // FC
UP_ROWS = D // NDEV
DOWN_ROWS = FF // NDEV
TB = 512


def dot_nn(a, b):
    return lax.dot_general(a, b, (((1,), (0,)), ((), ())), preferred_element_type=F32)


def dot_nt(a, b):
    return lax.dot_general(a, b, (((1,), (1,)), ((), ())), preferred_element_type=F32)


def dot_tn(a, b):
    return lax.dot_general(a, b, (((0,), (0,)), ((), ())), preferred_element_type=F32)


def gelu_half(h):
    u = h * h
    return u, 0.5 * jnp.tanh(h * (GELU_B * u + GELU_A)) + 0.5


def gelu_and_grad(h, grad_act):
    u, s = gelu_half(h)
    g = h * s
    slope = s + (g - g * s) * ((6.0 * GELU_B) * u + 2.0 * GELU_A)
    return g.astype(BF16), (grad_act * slope).astype(BF16)


def adam_math(grad_sum, acc, master, mom, vel):
    grad_mean = (acc + grad_sum) / MICROBATCHES
    mom = BETA_ONE * mom + (1.0 - BETA_ONE) * grad_mean
    vel = BETA_TWO * vel + (1.0 - BETA_TWO) * grad_mean * grad_mean
    step_dir = (mom / CORR_ONE) / (jnp.sqrt(vel / CORR_TWO) + ADAM_EPS)
    master = master - LEARN_RATE * (step_dir + WEIGHT_DECAY * master)
    return master, mom, vel


def step_kernel(x_saved, grad_out, x_next, w_up, w_down, acc_up, acc_dn, mas_up, mas_dn, mo_up, mo_dn, ve_up, ve_dn,
                o_mas_up, o_mas_dn, o_mo_up, o_mo_dn, o_ve_up, o_ve_dn, y_out,
                xs_top, xs_low, dyb, dxa, w1, w2, sent_up, sent_dn, recv_up, recv_dn,
                s_acc_up, s_mas_up, s_mo_up, s_ve_up,
                own_up, own_dn, acc1, acc2,
                load_sem, tok_send, tok_recv, rs_send, rs_recv, ag_send, ag_recv, out_sem, y_sem, free_sem):
    me = lax.axis_index('fsdp')
    stage = lax.rem(me, 2)
    other = 1 - stage
    chip = me // 2
    partner = me + 1 - 2 * stage

    def load(i, src, dst):
        return pltpu.make_async_copy(src, dst, load_sem.at[i])

    loads = [
        load(0, w_up.at[stage, 1], w1.at[1]),
        load(1, x_saved.at[stage, 1, 0], xs_top.at[0]),
        load(2, w_down.at[stage, 1], w2.at[1]),
        load(3, grad_out.at[stage, 0], dyb.at[0]),
        load(4, w_up.at[stage, 0], w1.at[0]),
        load(5, x_saved.at[stage, 0, 0], xs_low.at[0]),
        load(6, w_down.at[stage, 0], w2.at[0]),
        load(7, acc_up, s_acc_up), load(8, mas_up, s_mas_up), load(9, mo_up, s_mo_up), load(10, ve_up, s_ve_up),
    ]

    def dn_rows(layer, arr, st):
        return ((layer * 4 + arr) * 2 + st) * DOWN_ROWS

    def dn_view(layer, arr, st):
        return dxa.at[0, pl.ds(dn_rows(layer, arr, st), DOWN_ROWS), :]

    dn_loads = [load(11 + arr * 4 + layer * 2 + st, src.at[st, layer], dn_view(layer, arr, st))
                for arr, src in enumerate((acc_dn, mas_dn, mo_dn, ve_dn)) for layer in range(2) for st in range(2)]
    for c in loads[:4]:
        c.start()

    barrier = pltpu.get_barrier_semaphore()

    def greet(t, _):
        pl.semaphore_signal(barrier, inc=1, device_id=(lax.rem(me + t, NDEV),), device_id_type=MESH)
        return 0

    lax.fori_loop(1, NDEV, greet, 0)
    pl.semaphore_wait(barrier, NDEV - 1)

    def push(i, src, dst):
        return pltpu.make_async_remote_copy(src_ref=src, dst_ref=dst, send_sem=tok_send.at[i], recv_sem=tok_recv.at[i],
                                            device_id=(partner,), device_id_type=MESH)

    pushes = [
        push(0, x_saved.at[other, 1, 0], xs_top.at[1]),
        push(1, grad_out.at[other, 0], dyb.at[1]),
        push(2, x_saved.at[other, 0, 0], xs_low.at[1]),
        push(3, x_next.at[other, 0], xs_top.at[1]),
    ]
    for c in pushes[:3]:
        c.start()
    for c in loads[4:]:
        c.start()
    for c in loads[:4]:
        c.wait()

    def send_up(layer, chunk, dest):
        return pltpu.make_async_remote_copy(
            src_ref=sent_up.at[layer, chunk, pl.ds(pl.multiple_of(dest * UP_ROWS, UP_ROWS), UP_ROWS), :],
            dst_ref=recv_up.at[layer, me, chunk],
            send_sem=rs_send.at[layer, 0], recv_sem=rs_recv.at[layer, 0],
            device_id=(dest,), device_id_type=MESH)

    def send_dn(layer, chunk, core):
        dest = 2 * chunk + core
        return pltpu.make_async_remote_copy(
            src_ref=sent_dn.at[layer, dest],
            dst_ref=recv_dn.at[layer, me],
            send_sem=rs_send.at[layer, 1], recv_sem=rs_recv.at[layer, 1],
            device_id=(dest,), device_id_type=MESH)

    def backward(layer, xs, with_dx, first_waits):
        def chunk_body(t, _):
            chunk = lax.rem(chip + 1 + t, NCHUNK)
            cols = pl.ds(pl.multiple_of(chunk * FC, FC), FC)

            def token_body(q, _):
                @pl.when(jnp.logical_and(t == 0, q == 1))
                def _():
                    for c in first_waits:
                        c.wait_recv()

                @pl.when(q == 0)
                def _():
                    acc1[...] = jnp.zeros_like(acc1)
                    acc2[...] = jnp.zeros_like(acc2)

                x = xs[q]
                dy = dyb[q]
                hidden = dot_nn(x, w1[layer, :, cols])
                grad_act = dot_nt(dy, w2[layer, cols, :])
                act, grad_hidden = gelu_and_grad(hidden, grad_act)
                acc2[...] += dot_tn(act, dy)
                acc1[...] += dot_tn(x, grad_hidden)
                if with_dx:
                    part = dot_nt(grad_hidden, w1[layer, :, cols])

                    @pl.when(t == 0)
                    def _():
                        dxa[q] = part

                    @pl.when(t > 0)
                    def _():
                        dxa[q] += part
                return 0

            lax.fori_loop(0, 2, token_body, 0)
            sent_up[layer, chunk] = acc1[...].astype(BF16)
            for core in range(2):
                sent_dn[layer, 2 * chunk + core] = acc2[core * DOWN_ROWS:(core + 1) * DOWN_ROWS, :].astype(BF16)

            @pl.when(t < NCHUNK - 1)
            def _():
                send_dn(layer, chunk, 0).start()
                send_dn(layer, chunk, 1).start()

            @pl.when(t == NCHUNK - 1)
            def _():
                send_dn(layer, chunk, other).start()
                recv_dn[layer, me] = sent_dn[layer, me]

            def send_body(i, _):
                send_up(layer, chunk, lax.rem(me + i, NDEV)).start()
                return 0

            lax.fori_loop(1, NDEV, send_body, 0)
            recv_up[layer, me, chunk] = sent_up[layer, chunk, pl.ds(pl.multiple_of(me * UP_ROWS, UP_ROWS), UP_ROWS), :]
            return 0

        lax.fori_loop(0, NCHUNK, chunk_body, 0)

    backward(1, xs_top, True, pushes[:2])
    pl.semaphore_signal(free_sem, inc=1, device_id=(partner,), device_id_type=MESH)

    def cot_body(b, _):
        q = b // 4
        rows = pl.ds(pl.multiple_of(lax.rem(b, 4) * TB, TB), TB)
        dyb[q, rows, :] = (dyb[q, rows, :].astype(F32) + dxa[q, rows, :]).astype(BF16)
        return 0

    lax.fori_loop(0, 8, cot_body, 0)
    for c in dn_loads:
        c.start()
    for c in loads[4:7]:
        c.wait()
    backward(0, xs_low, False, pushes[2:3])

    own_next = load(1, x_next.at[stage, 0], xs_top.at[0])
    own_next.start()
    pl.semaphore_wait(free_sem, 1)
    pushes[0].wait_send()
    pushes[3].start()
    for c in loads[7:] + dn_loads:
        c.wait()

    def rs_wait(layer, mat):
        ref = (recv_up if mat == 0 else recv_dn).at[layer, pl.ds(0, NDEV - 1)]
        pltpu.make_async_copy(ref, ref, rs_recv.at[layer, mat]).wait()

    def adam_up(layer):
        def body(chunk, _):
            cols = pl.ds(pl.multiple_of(chunk * FC, FC), FC)
            for st in range(2):
                total = recv_up[layer, st, chunk].astype(F32)
                for k in range(1, 8):
                    total = total + recv_up[layer, 2 * k + st, chunk].astype(F32)
                new = adam_math(total, s_acc_up[st, layer, :, cols], s_mas_up[st, layer, :, cols],
                                s_mo_up[st, layer, :, cols], s_ve_up[st, layer, :, cols])
                s_mas_up[st, layer, :, cols] = new[0]
                s_mo_up[st, layer, :, cols] = new[1]
                s_ve_up[st, layer, :, cols] = new[2]
                own_up[layer, st, :, cols] = new[0].astype(BF16)
            return 0

        lax.fori_loop(0, NCHUNK, body, 0)

    def adam_dn(layer):
        def body(r, _):
            rows = pl.ds(pl.multiple_of(r * 16, 16), 16)
            for st in range(2):
                total = recv_dn[layer, st, rows, :].astype(F32)
                for k in range(1, 8):
                    total = total + recv_dn[layer, 2 * k + st, rows, :].astype(F32)
                at = [pl.ds(pl.multiple_of(dn_rows(layer, arr, st) + r * 16, 16), 16) for arr in range(4)]
                new = adam_math(total, *(dxa[0, a, :] for a in at))
                for a, val in zip(at[1:], new):
                    dxa[0, a, :] = val
                own_dn[layer, st, rows, :] = new[0].astype(BF16)
            return 0

        lax.fori_loop(0, DOWN_ROWS // 16, body, 0)

    pairs_up = ((s_mas_up, o_mas_up), (s_mo_up, o_mo_up), (s_ve_up, o_ve_up))

    def out_copies(layer, mat):
        if mat == 0:
            return [pltpu.make_async_copy(src.at[:, layer], dst.at[:, layer], out_sem.at[layer, 0, i])
                    for i, (src, dst) in enumerate(pairs_up)]
        return [pltpu.make_async_copy(dn_view(layer, i + 1, st), dst.at[st, layer], out_sem.at[layer, 1 + st, i])
                for i, dst in enumerate((o_mas_dn, o_mo_dn, o_ve_dn)) for st in range(2)]

    def gather(layer, mat):
        if mat == 0:
            rows = pl.ds(pl.multiple_of(me * UP_ROWS, UP_ROWS), UP_ROWS)
            own, full = own_up, w1
        else:
            rows = pl.ds(pl.multiple_of(me * DOWN_ROWS, DOWN_ROWS), DOWN_ROWS)
            own, full = own_dn, w2

        def body(i, _):
            dest = lax.rem(me + i, NDEV)
            pltpu.make_async_remote_copy(
                src_ref=own.at[layer, lax.rem(dest, 2)], dst_ref=full.at[layer, rows, :],
                send_sem=ag_send.at[layer, mat], recv_sem=ag_recv.at[layer, mat],
                device_id=(dest,), device_id_type=MESH).start()
            return 0

        lax.fori_loop(1, NDEV, body, 0)
        full[layer, rows, :] = own[layer, stage]

    def ag_ref(layer, mat):
        if mat == 0:
            return w1.at[layer, pl.ds(0, D - UP_ROWS), :]
        return w2.at[layer, pl.ds(0, FF - DOWN_ROWS), :]

    def ag_wait(layer, mat):
        ref = ag_ref(layer, mat)
        pltpu.make_async_copy(ref, ref, ag_recv.at[layer, mat]).wait()

    rs_wait(1, 0)
    adam_up(1)
    rs_wait(1, 1)
    adam_dn(1)
    rs_wait(0, 0)
    adam_up(0)
    gather(0, 0)
    rs_wait(0, 1)
    adam_dn(0)
    gather(0, 1)
    gather(1, 0)
    gather(1, 1)
    for layer in range(2):
        for mat in range(2):
            for c in out_copies(layer, mat):
                c.start()
    own_next.wait()
    pushes[3].wait_recv()

    def forward(layer, src, dst, last):
        ag_wait(layer, 0)
        ag_wait(layer, 1)

        def body(b, _):
            q = b // 4
            rows = pl.ds(pl.multiple_of(lax.rem(b, 4) * TB, TB), TB)
            x = src[q, rows, :]
            hidden = dot_nn(x, w1[layer])
            u, s = gelu_half(hidden)
            act = (hidden * s).astype(BF16)
            dst[q, rows, :] = (x.astype(F32) + dot_nn(act, w2[layer])).astype(BF16)
            if last:
                @pl.when(q == 0)
                def _():
                    pltpu.make_async_copy(dst.at[0, rows, :], y_out.at[stage, 0, rows, :], y_sem.at[0]).start()

                @pl.when(q == 1)
                def _():
                    pltpu.make_async_remote_copy(src_ref=dst.at[1, rows, :], dst_ref=y_out.at[stage, 0, rows, :],
                                                 send_sem=y_sem.at[1], recv_sem=y_sem.at[2],
                                                 device_id=(partner,), device_id_type=MESH).start()
            return 0

        lax.fori_loop(0, 8, body, 0)

    forward(0, xs_top, xs_low, False)
    forward(1, xs_low, dyb, True)

    for i in range(3):
        pltpu.make_async_copy(dyb.at[0], dyb.at[0], y_sem.at[i]).wait()
    for i in range(1, 4):
        pushes[i].wait_send()
    for layer in range(2):
        for mat in range(2):
            ref = (recv_up if mat == 0 else recv_dn).at[layer, pl.ds(0, NDEV - 1)]
            pltpu.make_async_copy(ref, ref, rs_send.at[layer, mat]).wait()
            ref = ag_ref(layer, mat)
            pltpu.make_async_copy(ref, ref, ag_send.at[layer, mat]).wait()
            for c in out_copies(layer, mat):
                c.wait()


def solution(mesh):
    tok_spec = P(None, 'fsdp')
    layer_spec = P(None, None, 'fsdp')
    rep_spec = P()
    any_spec = pl.BlockSpec(memory_space=pl.ANY)
    up_state = (2, 2, UP_ROWS, FF)
    dn_state = (2, 2, DOWN_ROWS, D)
    sds = jax.ShapeDtypeStruct
    dma = pltpu.SemaphoreType.DMA

    call = pl.pallas_call(
        step_kernel,
        out_shape=(sds(up_state, F32), sds(dn_state, F32)) * 3 + (sds((2, 1, SEQ, D), BF16),),
        in_specs=[any_spec] * 13,
        out_specs=(any_spec,) * 7,
        scratch_shapes=[
            pltpu.VMEM((2, SEQ, D), BF16), pltpu.VMEM((2, SEQ, D), BF16), pltpu.VMEM((2, SEQ, D), BF16),
            pltpu.VMEM((2, SEQ, D), F32),
            pltpu.VMEM((2, D, FF), BF16), pltpu.VMEM((2, FF, D), BF16),
            pltpu.VMEM((2, NCHUNK, D, FC), BF16), pltpu.VMEM((2, NDEV, DOWN_ROWS, D), BF16),
            pltpu.VMEM((2, NDEV, NCHUNK, UP_ROWS, FC), BF16), pltpu.VMEM((2, NDEV, DOWN_ROWS, D), BF16),
        ] + [pltpu.VMEM(up_state, F32)] * 4 + [
            pltpu.VMEM((2, 2, UP_ROWS, FF), BF16), pltpu.VMEM((2, 2, DOWN_ROWS, D), BF16),
            pltpu.VMEM((D, FC), F32), pltpu.VMEM((FC, D), F32),
            dma((27,)), dma((4,)), dma((4,)), dma((2, 2)), dma((2, 2)), dma((2, 2)), dma((2, 2)),
            dma((2, 3, 3)), dma((3,)), pltpu.SemaphoreType.REGULAR,
        ],
        compiler_params=pltpu.CompilerParams(collective_id=0, has_side_effects=True, vmem_limit_bytes=67043328),
    )

    def device_step(*args):
        return call(*args)

    return jax.shard_map(device_step, mesh=mesh, in_specs=(layer_spec, tok_spec, tok_spec, rep_spec, rep_spec) + (layer_spec,) * 8,
                         out_specs=(layer_spec,) * 6 + (tok_spec,), check_vma=False)
```

time: 588 us -> 283 us (0.48)
  Pallas kernels: 0 us -> 268 us
  matrix products: 261 us -> 0 us
  waiting for transfers between devices: 224 us -> 0 us
  other arithmetic: 44 us -> 0 us
  starting transfers between devices: 33.1 us -> 0 us
  between operations: 14.8 us -> 0.68 us
  local copies, waits for them, and re-layouts: 3.63 us -> 10.7 us
    pallas_call x0 -> x1, Pallas kernels: none -> 268 us  [device_step(): return call(*args)]
    dot_general x20 -> x0, matrix products: 261 us -> none  [the longest x4 62.8 us: backward_layer(): jnp.einsum('bsd,bsf->df', x_in, grad_hidden, preferred_element_type=jnp.f...]
    all_to_all x8 -> x0, waiting for transfers between devices: 126 us -> none  [scatter_sum(): lax.all_to_all(part.astype(jnp.bfloat16), 'fsdp', 0, 0, tiled=True)]
    all_gather x8 -> x0, waiting for transfers between devices: 95.7 us -> none  [the longest x4 48.5 us: device_step(): lax.all_gather(new_up[0].astype(jnp.bfloat16), 'fsdp', axis=0, tiled=True)]
    all_to_all x8 -> x0, starting transfers between devices: 32.6 us -> none  [scatter_sum(): lax.all_to_all(part.astype(jnp.bfloat16), 'fsdp', 0, 0, tiled=True)]
    another operation x13 -> x0, other arithmetic: 14.5 us -> none  [the longest x12 10.5 us: device_step(): jnp.stack(entry)]
    sub x4 -> x0, other arithmetic: 11.2 us -> none  [adam_update(): master = master - LEARN_RATE * (step_dir + WEIGHT_DECAY * master)]
    reduce_sum x8 -> x0, other arithmetic: 9.84 us -> none  [scatter_sum(): jnp.sum(received.reshape((groups, -1) + received.shape[1:]), axis=0, dtyp...]
  transfers between devices with their start and end apart: 16 -> 0, of which waited for: 12 -> 0; matrix products, arithmetic and copies ran while one was open for 43% -> 0% of each run, Pallas kernels for 0% -> 0%
where the time goes in v1:
time: 283 us; the launch traced here: 279 us
  Pallas kernels  268 us (95%)
  local copies, waits for them, and re-layouts  10.7 us (4%)
    pallas_call x1, Pallas kernels, device_step(): return call(*args)  268 us
    unnamed x17, local copies, waits for them, and re-layouts  10.7 us

profile of v1, /device:TPU:0, one launch (start us, length us, event | category | flops | bytes accessed | tf_op | source)
XLA Modules:
  0.0 279.2 jit_solution(6994247291545833334)
XLA Ops:
  0.6 267.8 %shard_map.180 = (f32[2,2,32,2048]{3,2,1,0:T(8,128)}, f32[2,2,128,512]{3,2,1,0:T(8,128)}, f32[2,2,32,2048]{3,2,1,0:T(8,128)}, f32[2,2,128,512]{3,2,1,0:T(8,128)}...) custom-call(bf16[2,2,1,2048,512]{4,3,2,1,0:T(8,128)(2,1)} %x_saved.1, ...), custom_call_target="tpu_custom_call" | custom-call | tf_op jit(solution)/shard_map/pallas_call | solution.py:398
  268.4 0.0 copy-start.4
  268.4 0.0 copy-start.3
  268.4 0.0 copy-start.2
  268.4 2.4 copy.27
  270.9 0.0 copy-start.1
  270.9 2.4 copy.28
  273.2 0.0 copy-done.4
  273.2 0.0 copy-start
  273.2 1.0 copy.29
  274.2 0.0 copy-done.3
  274.2 1.0 copy.30
  275.2 0.0 copy-done.2
  275.2 1.0 copy.31
  276.2 0.0 copy-done.1
  276.2 1.0 copy.32
  277.1 0.0 copy-done
  277.1 2.0 copy.33
Async XLA Ops:
  268.4 4.8 %copy-start.4 = (f32[2,2,32,2048]{3,2,1,0:T(8,128)S(1)}, f32[2,2,32,2048]{3,2,1,0:T(8,128)}, u32[]{:S(2)}) copy-start(f32[2,2,32,2048]{3,2,1,0:T(8,128)} %get-tuple-element.16) | copy-start | bytes 3145732
  268.4 5.8 %copy-start.3 = (f32[2,2,128,512]{3,2,1,0:T(8,128)S(1)}, f32[2,2,128,512]{3,2,1,0:T(8,128)}, u32[]{:S(2)}) copy-start(f32[2,2,128,512]{3,2,1,0:T(8,128)} %get-tuple-element.17) | copy-start | bytes 3145732
  268.4 6.8 %copy-start.2 = (f32[2,2,32,2048]{3,2,1,0:T(8,128)S(1)}, f32[2,2,32,2048]{3,2,1,0:T(8,128)}, u32[]{:S(2)}) copy-start(f32[2,2,32,2048]{3,2,1,0:T(8,128)} %get-tuple-element.18) | copy-start | bytes 3145732
  270.9 5.3 %copy-start.1 = (f32[2,2,128,512]{3,2,1,0:T(8,128)S(1)}, f32[2,2,128,512]{3,2,1,0:T(8,128)}, u32[]{:S(2)}) copy-start(f32[2,2,128,512]{3,2,1,0:T(8,128)} %get-tuple-element.19) | copy-start | bytes 3145732
  273.2 3.9 %copy-start = (bf16[2,1,2048,512]{3,2,1,0:T(8,128)(2,1)S(1)}, bf16[2,1,2048,512]{3,2,1,0:T(8,128)(2,1)}, u32[]{:S(2)}) copy-start(bf16[2,1,2048,512]{3,2,1,0:T(8,128)(2,1)} %get-tuple-element.20) | copy-start | bytes 12582916

commit v2 on v1

--- a/solution.py
+++ b/solution.py
@@ -77,6 +77,15 @@
     other = 1 - stage
     chip = me // 2
     partner = me + 1 - 2 * stage
+
+    bits = (lax.rem(chip, 2), lax.rem(chip // 2, 2), chip // 4)
+
+    def chip_xor(mask):
+        flips = (lax.rem(mask, 2), lax.rem(mask // 2, 2), mask // 4)
+        return sum(lax.rem(b + f, 2) * w for b, f, w in zip(bits, flips, (1, 2, 4)))
+
+    def chip_at(mask):
+        return sum(((1 - b) if mask & w else b) * w for b, w in zip(bits, (1, 2, 4)))
 
     def load(i, src, dst):
         return pltpu.make_async_copy(src, dst, load_sem.at[i])
@@ -146,7 +155,7 @@
 
     def backward(layer, xs, with_dx, first_waits):
         def chunk_body(t, _):
-            chunk = lax.rem(chip + 1 + t, NCHUNK)
+            chunk = chip_xor(NCHUNK - 1 - t)
             cols = pl.ds(pl.multiple_of(chunk * FC, FC), FC)
 
             def token_body(q, _):
@@ -195,7 +204,7 @@
                 recv_dn[layer, me] = sent_dn[layer, me]
 
             def send_body(i, _):
-                send_up(layer, chunk, lax.rem(me + i, NDEV)).start()
+                send_up(layer, chunk, 2 * chip_xor((NDEV - i) // 2) + lax.rem(stage + NDEV - i, 2)).start()
                 return 0
 
             lax.fori_loop(1, NDEV, send_body, 0)
@@ -274,24 +283,50 @@
         return [pltpu.make_async_copy(dn_view(layer, i + 1, st), dst.at[st, layer], out_sem.at[layer, 1 + st, i])
                 for i, dst in enumerate((o_mas_dn, o_mo_dn, o_ve_dn)) for st in range(2)]
 
-    def gather(layer, mat):
+    def piece_rows(layer, mat, dev):
         if mat == 0:
-            rows = pl.ds(pl.multiple_of(me * UP_ROWS, UP_ROWS), UP_ROWS)
-            own, full = own_up, w1
-        else:
-            rows = pl.ds(pl.multiple_of(me * DOWN_ROWS, DOWN_ROWS), DOWN_ROWS)
-            own, full = own_dn, w2
-
-        def body(i, _):
-            dest = lax.rem(me + i, NDEV)
-            pltpu.make_async_remote_copy(
-                src_ref=own.at[layer, lax.rem(dest, 2)], dst_ref=full.at[layer, rows, :],
-                send_sem=ag_send.at[layer, mat], recv_sem=ag_recv.at[layer, mat],
-                device_id=(dest,), device_id_type=MESH).start()
-            return 0
-
-        lax.fori_loop(1, NDEV, body, 0)
-        full[layer, rows, :] = own[layer, stage]
+            return w1.at[layer, pl.ds(pl.multiple_of(dev * UP_ROWS, UP_ROWS), UP_ROWS), :]
+        return w2.at[layer, pl.ds(pl.multiple_of(dev * DOWN_ROWS, DOWN_ROWS), DOWN_ROWS), :]
+
+    def unit_rows(layer, mat, owner, part=None):
+        full, size, cuts = ((w1, 2 * UP_ROWS, (0, 32, 48, 64)), (w2, 2 * DOWN_ROWS, (0, 96, 176, 256)))[mat]
+        lo, hi = (0, size) if part is None else cuts[part:part + 2]
+        return full.at[layer, pl.ds(pl.multiple_of(owner * size + lo, 16), hi - lo), :]
+
+    def ag_copy(layer, mat, src, dst, slot, dest):
+        return pltpu.make_async_remote_copy(src_ref=src, dst_ref=dst, send_sem=ag_send.at[layer, mat],
+                                            recv_sem=ag_recv.at[layer, mat, slot],
+                                            device_id=(dest,), device_id_type=MESH)
+
+    def ag_got(layer, mat, slot, ref):
+        pltpu.make_async_copy(ref, ref, ag_recv.at[layer, mat, slot]).wait()
+
+    def round0(layer, mat):
+        own = (own_up, own_dn)[mat]
+        ag_copy(layer, mat, own.at[layer, other], piece_rows(layer, mat, me), 0, partner).start()
+        piece_rows(layer, mat, me)[...] = own[layer, stage]
+
+    def neighbour(mask):
+        return 2 * chip_at(mask) + stage
+
+    def send_unit(layer, mat, owner, slot, mask, part=None):
+        ref = unit_rows(layer, mat, chip_at(owner), part)
+        ag_copy(layer, mat, ref, ref, slot, neighbour(mask)).start()
+
+    def round1(layer, mat):
+        ag_got(layer, mat, 0, piece_rows(layer, mat, partner))
+        for i in range(3):
+            send_unit(layer, mat, 0, 1 + i, 1 << i)
+
+    def round2(layer, mat):
+        for link, came in ((0, 1), (1, 2), (2, 0)):
+            ag_got(layer, mat, 1 + came, unit_rows(layer, mat, chip_at(1 << came)))
+            send_unit(layer, mat, 1 << came, 4 + link, 1 << link)
+
+    def round3(layer, mat):
+        for link, owner, came in ((2, 3, 0), (0, 6, 1), (1, 5, 2)):
+            ag_got(layer, mat, 4 + came, unit_rows(layer, mat, chip_at(owner)))
+            send_unit(layer, mat, owner, 7, 1 << link, link)
 
     def ag_ref(layer, mat):
         if mat == 0:
@@ -299,8 +334,7 @@
         return w2.at[layer, pl.ds(0, FF - DOWN_ROWS), :]
 
     def ag_wait(layer, mat):
-        ref = ag_ref(layer, mat)
-        pltpu.make_async_copy(ref, ref, ag_recv.at[layer, mat]).wait()
+        ag_got(layer, mat, 7, unit_rows(layer, mat, chip_at(7)))
 
     rs_wait(1, 0)
     adam_up(1)
@@ -308,12 +342,20 @@
     adam_dn(1)
     rs_wait(0, 0)
     adam_up(0)
-    gather(0, 0)
+    round0(0, 0)
     rs_wait(0, 1)
     adam_dn(0)
-    gather(0, 1)
-    gather(1, 0)
-    gather(1, 1)
+    round0(0, 1)
+    round1(0, 0)
+    round1(0, 1)
+    round0(1, 0)
+    round0(1, 1)
+    round2(0, 0)
+    round2(0, 1)
+    round3(0, 0)
+    round1(1, 0)
+    round3(0, 1)
+    round1(1, 1)
     for layer in range(2):
         for mat in range(2):
             for c in out_copies(layer, mat):
@@ -333,6 +375,11 @@
             u, s = gelu_half(hidden)
             act = (hidden * s).astype(BF16)
             dst[q, rows, :] = (x.astype(F32) + dot_nn(act, w2[layer])).astype(BF16)
+            if not last:
+                for at, step, mat in ((1, round2, 0), (3, round2, 1), (5, round3, 0), (7, round3, 1)):
+                    @pl.when(b == at)
+                    def _(step=step, mat=mat):
+                        step(1, mat)
             if last:
                 @pl.when(q == 0)
                 def _():
@@ -388,7 +435,7 @@
         ] + [pltpu.VMEM(up_state, F32)] * 4 + [
             pltpu.VMEM((2, 2, UP_ROWS, FF), BF16), pltpu.VMEM((2, 2, DOWN_ROWS, D), BF16),
             pltpu.VMEM((D, FC), F32), pltpu.VMEM((FC, D), F32),
-            dma((27,)), dma((4,)), dma((4,)), dma((2, 2)), dma((2, 2)), dma((2, 2)), dma((2, 2)),
+            dma((27,)), dma((4,)), dma((4,)), dma((2, 2)), dma((2, 2)), dma((2, 2)), dma((2, 2, 8)),
             dma((2, 3, 3)), dma((3,)), pltpu.SemaphoreType.REGULAR,
         ],
         compiler_params=pltpu.CompilerParams(collective_id=0, has_side_effects=True, vmem_limit_bytes=67043328),

time: 283 us -> 231 us (0.82); the launches traced: 279 us -> 231 us
  Pallas kernels: 268 us -> 219 us
    pallas_call x1, Pallas kernels: 268 us -> 219 us  [device_step(): return call(*args)]
where the time goes in v2:
time: 231 us
  Pallas kernels  219 us (95%)
  local copies, waits for them, and re-layouts  10.7 us (5%)
    pallas_call x1, Pallas kernels, device_step(): return call(*args)  219 us
    unnamed x17, local copies, waits for them, and re-layouts  10.7 us

profile of v2, /device:TPU:0, one launch (start us, length us, event | category | flops | bytes accessed | tf_op | source)
XLA Modules:
  0.0 230.6 jit_solution(17096490353743826669)
XLA Ops:
  0.6 219.2 %shard_map.180 = (f32[2,2,32,2048]{3,2,1,0:T(8,128)}, f32[2,2,128,512]{3,2,1,0:T(8,128)}, f32[2,2,32,2048]{3,2,1,0:T(8,128)}, f32[2,2,128,512]{3,2,1,0:T(8,128)}...) custom-call(bf16[2,2,1,2048,512]{4,3,2,1,0:T(8,128)(2,1)} %x_saved.1, ...), custom_call_target="tpu_custom_call" | custom-call | tf_op jit(solution)/shard_map/pallas_call | solution.py:445
  219.8 0.0 copy-start.4
  219.8 0.0 copy-start.3
  219.8 0.0 copy-start.2
  219.8 2.4 %copy.27 = f32[2,2,32,2048]{3,2,1,0:T(8,128)} copy(f32[2,2,32,2048]{3,2,1,0:T(8,128)} %get-tuple-element.14) | data formatting | bytes 2097152
  222.3 0.0 copy-start.1
  222.3 2.4 %copy.28 = f32[2,2,128,512]{3,2,1,0:T(8,128)} copy(f32[2,2,128,512]{3,2,1,0:T(8,128)} %get-tuple-element.15) | data formatting | bytes 2097152
  224.6 0.0 copy-done.4
  224.7 0.0 copy-start
  224.7 1.0 copy.29
  225.6 0.0 copy-done.3
  225.6 1.0 copy.30
  226.6 0.0 copy-done.2
  226.6 1.0 copy.31
  227.6 0.0 copy-done.1
  227.6 1.0 copy.32
  228.5 0.0 copy-done
  228.5 2.0 copy.33
Async XLA Ops:
  219.8 4.8 %copy-start.4 = (f32[2,2,32,2048]{3,2,1,0:T(8,128)S(1)}, f32[2,2,32,2048]{3,2,1,0:T(8,128)}, u32[]{:S(2)}) copy-start(f32[2,2,32,2048]{3,2,1,0:T(8,128)} %get-tuple-element.16) | copy-start | bytes 3145732
  219.8 5.8 %copy-start.3 = (f32[2,2,128,512]{3,2,1,0:T(8,128)S(1)}, f32[2,2,128,512]{3,2,1,0:T(8,128)}, u32[]{:S(2)}) copy-start(f32[2,2,128,512]{3,2,1,0:T(8,128)} %get-tuple-element.17) | copy-start | bytes 3145732
  219.8 6.8 %copy-start.2 = (f32[2,2,32,2048]{3,2,1,0:T(8,128)S(1)}, f32[2,2,32,2048]{3,2,1,0:T(8,128)}, u32[]{:S(2)}) copy-start(f32[2,2,32,2048]{3,2,1,0:T(8,128)} %get-tuple-element.18) | copy-start | bytes 3145732
  222.3 5.3 %copy-start.1 = (f32[2,2,128,512]{3,2,1,0:T(8,128)S(1)}, f32[2,2,128,512]{3,2,1,0:T(8,128)}, u32[]{:S(2)}) copy-start(f32[2,2,128,512]{3,2,1,0:T(8,128)} %get-tuple-element.19) | copy-start | bytes 3145732
  224.7 3.9 %copy-start = (bf16[2,1,2048,512]{3,2,1,0:T(8,128)(2,1)S(1)}, bf16[2,1,2048,512]{3,2,1,0:T(8,128)(2,1)}, u32[]{:S(2)}) copy-start(bf16[2,1,2048,512]{3,2,1,0:T(8,128)(2,1)} %get-tuple-element.20) | copy-start | bytes 12582916

commit v3 on v2

--- a/solution.py
+++ b/solution.py
@@ -30,7 +30,38 @@
 NCHUNK = FF // FC
 UP_ROWS = D // NDEV
 DOWN_ROWS = FF // NDEV
-TB = 512
+TB = 1024
+SUB = 1024
+ARRIVAL = (0, 1, 2, 4, 3, 6, 5, 7)
+ORDER = (7, 6, 5, 3, 1, 2, 4, 0)
+
+
+def PRE(r1, r2, r3):
+    return [(r1, 1, 0)]
+
+
+def MID(r1, r2, r3):
+    return [(r2, 0, 0), (r1, 0, 1), (r3, 0, 0)]
+
+
+def BEFORE1A(r1, r2, r3):
+    return [(r2, 0, 1)]
+
+
+def HOOKS1A(r1, r2, r3):
+    return {1: [(r2, 1, 0)], 2: [(r3, 0, 1)]}
+
+
+def HOOKS1B(r1, r2, r3):
+    return {1: [(r1, 1, 1)], 2: [(r3, 1, 0)]}
+
+
+def BEFORE2A(r1, r2, r3):
+    return [(r2, 1, 1)]
+
+
+def HOOKS2A(r1, r2, r3):
+    return {3: [(r3, 1, 1)]}
 
 
 def dot_nn(a, b):
@@ -70,7 +101,7 @@
                 o_mas_up, o_mas_dn, o_mo_up, o_mo_dn, o_ve_up, o_ve_dn, y_out,
                 xs_top, xs_low, dyb, dxa, w1, w2, sent_up, sent_dn, recv_up, recv_dn,
                 s_acc_up, s_mas_up, s_mo_up, s_ve_up,
-                own_up, own_dn, acc1, acc2,
+                own_up, own_dn, acc1, acc2, act_buf, dh_buf,
                 load_sem, tok_send, tok_recv, rs_send, rs_recv, ag_send, ag_recv, out_sem, y_sem, free_sem):
     me = lax.axis_index('fsdp')
     stage = lax.rem(me, 2)
@@ -83,6 +114,9 @@
     def chip_xor(mask):
         flips = (lax.rem(mask, 2), lax.rem(mask // 2, 2), mask // 4)
         return sum(lax.rem(b + f, 2) * w for b, f, w in zip(bits, flips, (1, 2, 4)))
+
+    def pick(table, i):
+        return sum(jnp.where(i == k, v, 0) for k, v in enumerate(table))
 
     def chip_at(mask):
         return sum(((1 - b) if mask & w else b) * w for b, w in zip(bits, (1, 2, 4)))
@@ -138,24 +172,29 @@
     for c in loads[:4]:
         c.wait()
 
+    def down_rows(dev):
+        return pl.ds(pl.multiple_of(dev * DOWN_ROWS, DOWN_ROWS), DOWN_ROWS)
+
     def send_up(layer, chunk, dest):
         return pltpu.make_async_remote_copy(
             src_ref=sent_up.at[layer, chunk, pl.ds(pl.multiple_of(dest * UP_ROWS, UP_ROWS), UP_ROWS), :],
-            dst_ref=recv_up.at[layer, me, chunk],
+            dst_ref=recv_up.at[layer, chunk, pl.ds(pl.multiple_of(me * UP_ROWS, UP_ROWS), UP_ROWS), :],
             send_sem=rs_send.at[layer, 0], recv_sem=rs_recv.at[layer, 0],
             device_id=(dest,), device_id_type=MESH)
 
     def send_dn(layer, chunk, core):
         dest = 2 * chunk + core
         return pltpu.make_async_remote_copy(
-            src_ref=sent_dn.at[layer, dest],
-            dst_ref=recv_dn.at[layer, me],
+            src_ref=sent_dn.at[layer, down_rows(dest), :],
+            dst_ref=recv_dn.at[layer, down_rows(me), :],
             send_sem=rs_send.at[layer, 1], recv_sem=rs_recv.at[layer, 1],
             device_id=(dest,), device_id_type=MESH)
 
+    up_dests = [2 * chip_at(m) + core for m in ORDER[:-1] for core in range(2)] + [partner]
+
     def backward(layer, xs, with_dx, first_waits):
         def chunk_body(t, _):
-            chunk = chip_xor(NCHUNK - 1 - t)
+            chunk = chip_xor(pick(ORDER, t))
             cols = pl.ds(pl.multiple_of(chunk * FC, FC), FC)
 
             def token_body(q, _):
@@ -171,9 +210,13 @@
 
                 x = xs[q]
                 dy = dyb[q]
-                hidden = dot_nn(x, w1[layer, :, cols])
-                grad_act = dot_nt(dy, w2[layer, cols, :])
-                act, grad_hidden = gelu_and_grad(hidden, grad_act)
+                for lo in range(0, SEQ, SUB):
+                    part_rows = slice(lo, lo + SUB)
+                    hidden = dot_nn(x[part_rows], w1[layer, :, cols])
+                    grad_act = dot_nt(dy[part_rows], w2[layer, cols, :])
+                    act_buf[part_rows, :], dh_buf[part_rows, :] = gelu_and_grad(hidden, grad_act)
+                act = act_buf[...]
+                grad_hidden = dh_buf[...]
                 acc2[...] += dot_tn(act, dy)
                 acc1[...] += dot_tn(x, grad_hidden)
                 if with_dx:
@@ -190,8 +233,7 @@
 
             lax.fori_loop(0, 2, token_body, 0)
             sent_up[layer, chunk] = acc1[...].astype(BF16)
-            for core in range(2):
-                sent_dn[layer, 2 * chunk + core] = acc2[core * DOWN_ROWS:(core + 1) * DOWN_ROWS, :].astype(BF16)
+            sent_dn[layer, cols, :] = acc2[...].astype(BF16)
 
             @pl.when(t < NCHUNK - 1)
             def _():
@@ -201,14 +243,12 @@
             @pl.when(t == NCHUNK - 1)
             def _():
                 send_dn(layer, chunk, other).start()
-                recv_dn[layer, me] = sent_dn[layer, me]
-
-            def send_body(i, _):
-                send_up(layer, chunk, 2 * chip_xor((NDEV - i) // 2) + lax.rem(stage + NDEV - i, 2)).start()
-                return 0
-
-            lax.fori_loop(1, NDEV, send_body, 0)
-            recv_up[layer, me, chunk] = sent_up[layer, chunk, pl.ds(pl.multiple_of(me * UP_ROWS, UP_ROWS), UP_ROWS), :]
+                recv_dn[layer, down_rows(me), :] = sent_dn[layer, down_rows(me), :]
+
+            for dest in up_dests:
+                send_up(layer, chunk, dest).start()
+            own_rows = pl.ds(pl.multiple_of(me * UP_ROWS, UP_ROWS), UP_ROWS)
+            recv_up[layer, chunk, own_rows, :] = sent_up[layer, chunk, own_rows, :]
             return 0
 
         lax.fori_loop(0, NCHUNK, chunk_body, 0)
@@ -216,13 +256,15 @@
     backward(1, xs_top, True, pushes[:2])
     pl.semaphore_signal(free_sem, inc=1, device_id=(partner,), device_id_type=MESH)
 
+    def token_rows(b):
+        return b // 2, pl.ds(pl.multiple_of(lax.rem(b, 2) * TB, TB), TB)
+
     def cot_body(b, _):
-        q = b // 4
-        rows = pl.ds(pl.multiple_of(lax.rem(b, 4) * TB, TB), TB)
+        q, rows = token_rows(b)
         dyb[q, rows, :] = (dyb[q, rows, :].astype(F32) + dxa[q, rows, :]).astype(BF16)
         return 0
 
-    lax.fori_loop(0, 8, cot_body, 0)
+    lax.fori_loop(0, 4, cot_body, 0)
     for c in dn_loads:
         c.start()
     for c in loads[4:7]:
@@ -237,17 +279,22 @@
     for c in loads[7:] + dn_loads:
         c.wait()
 
+    def rs_ref(layer, mat):
+        if mat == 0:
+            return recv_up.at[layer, :, pl.ds(0, D - UP_ROWS), :]
+        return recv_dn.at[layer, pl.ds(0, FF - DOWN_ROWS), :]
+
     def rs_wait(layer, mat):
-        ref = (recv_up if mat == 0 else recv_dn).at[layer, pl.ds(0, NDEV - 1)]
+        ref = rs_ref(layer, mat)
         pltpu.make_async_copy(ref, ref, rs_recv.at[layer, mat]).wait()
 
     def adam_up(layer):
         def body(chunk, _):
             cols = pl.ds(pl.multiple_of(chunk * FC, FC), FC)
             for st in range(2):
-                total = recv_up[layer, st, chunk].astype(F32)
+                total = recv_up[layer, chunk, pl.ds(st * UP_ROWS, UP_ROWS), :].astype(F32)
                 for k in range(1, 8):
-                    total = total + recv_up[layer, 2 * k + st, chunk].astype(F32)
+                    total = total + recv_up[layer, chunk, pl.ds((2 * k + st) * UP_ROWS, UP_ROWS), :].astype(F32)
                 new = adam_math(total, s_acc_up[st, layer, :, cols], s_mas_up[st, layer, :, cols],
                                 s_mo_up[st, layer, :, cols], s_ve_up[st, layer, :, cols])
                 s_mas_up[st, layer, :, cols] = new[0]
@@ -262,9 +309,10 @@
         def body(r, _):
             rows = pl.ds(pl.multiple_of(r * 16, 16), 16)
             for st in range(2):
-                total = recv_dn[layer, st, rows, :].astype(F32)
+                from_dev = [pl.ds(pl.multiple_of((2 * k + st) * DOWN_ROWS + r * 16, 16), 16) for k in range(8)]
+                total = recv_dn[layer, from_dev[0], :].astype(F32)
                 for k in range(1, 8):
-                    total = total + recv_dn[layer, 2 * k + st, rows, :].astype(F32)
+                    total = total + recv_dn[layer, from_dev[k], :].astype(F32)
                 at = [pl.ds(pl.multiple_of(dn_rows(layer, arr, st) + r * 16, 16), 16) for arr in range(4)]
                 new = adam_math(total, *(dxa[0, a, :] for a in at))
                 for a, val in zip(at[1:], new):
@@ -336,51 +384,37 @@
     def ag_wait(layer, mat):
         ag_got(layer, mat, 7, unit_rows(layer, mat, chip_at(7)))
 
-    rs_wait(1, 0)
-    adam_up(1)
-    rs_wait(1, 1)
-    adam_dn(1)
-    rs_wait(0, 0)
-    adam_up(0)
-    round0(0, 0)
-    rs_wait(0, 1)
-    adam_dn(0)
-    round0(0, 1)
-    round1(0, 0)
-    round1(0, 1)
-    round0(1, 0)
-    round0(1, 1)
-    round2(0, 0)
-    round2(0, 1)
-    round3(0, 0)
-    round1(1, 0)
-    round3(0, 1)
-    round1(1, 1)
-    for layer in range(2):
-        for mat in range(2):
-            for c in out_copies(layer, mat):
-                c.start()
-    own_next.wait()
-    pushes[3].wait_recv()
-
-    def forward(layer, src, dst, last):
-        ag_wait(layer, 0)
-        ag_wait(layer, 1)
+    def run(calls):
+        for fn, *where in calls:
+            fn(*where)
+
+    def hooked(b, hooks):
+        for at, calls in hooks.items():
+            @pl.when(b == at)
+            def _(calls=calls):
+                run(calls)
+
+    def feature_rows(pos):
+        return pl.ds(pl.multiple_of(chip_at(ARRIVAL[pos]) * FC, FC), FC)
+
+    def forward_pass(layer, src, dst, lo, hi, hooks):
+        final = layer == 1 and hi == NCHUNK
 
         def body(b, _):
-            q = b // 4
-            rows = pl.ds(pl.multiple_of(lax.rem(b, 4) * TB, TB), TB)
+            hooked(b, hooks)
+            q, rows = token_rows(b)
             x = src[q, rows, :]
-            hidden = dot_nn(x, w1[layer])
+            hidden = dot_nn(x, jnp.concatenate([w1[layer, :, feature_rows(pos)] for pos in range(lo, hi)], axis=1))
             u, s = gelu_half(hidden)
-            act = (hidden * s).astype(BF16)
-            dst[q, rows, :] = (x.astype(F32) + dot_nn(act, w2[layer])).astype(BF16)
-            if not last:
-                for at, step, mat in ((1, round2, 0), (3, round2, 1), (5, round3, 0), (7, round3, 1)):
-                    @pl.when(b == at)
-                    def _(step=step, mat=mat):
-                        step(1, mat)
-            if last:
+            part = dot_nn((hidden * s).astype(BF16),
+                          jnp.concatenate([w2[layer, feature_rows(pos), :] for pos in range(lo, hi)], axis=0))
+            if lo > 0:
+                part = part + dxa[q, rows, :]
+            if hi < NCHUNK:
+                dxa[q, rows, :] = part
+            else:
+                dst[q, rows, :] = (x.astype(F32) + part).astype(BF16)
+            if final:
                 @pl.when(q == 0)
                 def _():
                     pltpu.make_async_copy(dst.at[0, rows, :], y_out.at[stage, 0, rows, :], y_sem.at[0]).start()
@@ -392,10 +426,44 @@
                                                  device_id=(partner,), device_id_type=MESH).start()
             return 0
 
-        lax.fori_loop(0, 8, body, 0)
-
-    forward(0, xs_top, xs_low, False)
-    forward(1, xs_low, dyb, True)
+        lax.fori_loop(0, 4, body, 0)
+
+    r1, r2, r3 = round1, round2, round3
+
+    rs_wait(1, 0)
+    adam_up(1)
+    round0(1, 0)
+    rs_wait(1, 1)
+    adam_dn(1)
+    round0(1, 1)
+    run(PRE(r1, r2, r3))
+    rs_wait(0, 0)
+    adam_up(0)
+    round0(0, 0)
+    rs_wait(0, 1)
+    round1(0, 0)
+    adam_dn(0)
+    round0(0, 1)
+    for layer in range(2):
+        for mat in range(2):
+            for c in out_copies(layer, mat):
+                c.start()
+    run(MID(r1, r2, r3))
+    own_next.wait()
+    pushes[3].wait_recv()
+    for layer in range(2):
+        for c in out_copies(layer, 1):
+            c.wait()
+    ag_wait(0, 0)
+    run(BEFORE1A(r1, r2, r3))
+    forward_pass(0, xs_top, xs_low, 0, 4, HOOKS1A(r1, r2, r3))
+    ag_wait(0, 1)
+    forward_pass(0, xs_top, xs_low, 4, 8, HOOKS1B(r1, r2, r3))
+    run(BEFORE2A(r1, r2, r3))
+    ag_wait(1, 0)
+    forward_pass(1, xs_low, dyb, 0, 4, HOOKS2A(r1, r2, r3))
+    ag_wait(1, 1)
+    forward_pass(1, xs_low, dyb, 4, 8, {})
 
     for i in range(3):
         pltpu.make_async_copy(dyb.at[0], dyb.at[0], y_sem.at[i]).wait()
@@ -403,12 +471,28 @@
         pushes[i].wait_send()
     for layer in range(2):
         for mat in range(2):
-            ref = (recv_up if mat == 0 else recv_dn).at[layer, pl.ds(0, NDEV - 1)]
+            ref = rs_ref(layer, mat)
             pltpu.make_async_copy(ref, ref, rs_send.at[layer, mat]).wait()
             ref = ag_ref(layer, mat)
             pltpu.make_async_copy(ref, ref, ag_send.at[layer, mat]).wait()
-            for c in out_copies(layer, mat):
-                c.wait()
+            if mat == 0:
+                for c in out_copies(layer, mat):
+                    c.wait()
+
+
+def emit_kernel(*refs):
+    src, dst, buf = refs[:7], refs[7:14], refs[14:21]
+    in_sem, done_sem = refs[21:]
+    spots = [(i, half) for i in range(7) for half in range(2)]
+    into = [pltpu.make_async_copy(src[i].at[h], buf[i].at[h], in_sem.at[i, h]) for i, h in spots]
+    out = [pltpu.make_async_copy(buf[i].at[h], dst[i].at[h], done_sem.at[i, h]) for i, h in spots]
+    for c in into:
+        c.start()
+    for c, d in zip(into, out):
+        c.wait()
+        d.start()
+    for d in out:
+        d.wait()
 
 
 def solution(mesh):
@@ -430,19 +514,30 @@
             pltpu.VMEM((2, SEQ, D), BF16), pltpu.VMEM((2, SEQ, D), BF16), pltpu.VMEM((2, SEQ, D), BF16),
             pltpu.VMEM((2, SEQ, D), F32),
             pltpu.VMEM((2, D, FF), BF16), pltpu.VMEM((2, FF, D), BF16),
-            pltpu.VMEM((2, NCHUNK, D, FC), BF16), pltpu.VMEM((2, NDEV, DOWN_ROWS, D), BF16),
-            pltpu.VMEM((2, NDEV, NCHUNK, UP_ROWS, FC), BF16), pltpu.VMEM((2, NDEV, DOWN_ROWS, D), BF16),
+            pltpu.VMEM((2, NCHUNK, D, FC), BF16), pltpu.VMEM((2, FF, D), BF16),
+            pltpu.VMEM((2, NCHUNK, D, FC), BF16), pltpu.VMEM((2, FF, D), BF16),
         ] + [pltpu.VMEM(up_state, F32)] * 4 + [
             pltpu.VMEM((2, 2, UP_ROWS, FF), BF16), pltpu.VMEM((2, 2, DOWN_ROWS, D), BF16),
             pltpu.VMEM((D, FC), F32), pltpu.VMEM((FC, D), F32),
+            pltpu.VMEM((SEQ, FC), BF16), pltpu.VMEM((SEQ, FC), BF16),
             dma((27,)), dma((4,)), dma((4,)), dma((2, 2)), dma((2, 2)), dma((2, 2)), dma((2, 2, 8)),
             dma((2, 3, 3)), dma((3,)), pltpu.SemaphoreType.REGULAR,
         ],
         compiler_params=pltpu.CompilerParams(collective_id=0, has_side_effects=True, vmem_limit_bytes=67043328),
     )
 
+    emit = pl.pallas_call(
+        emit_kernel,
+        out_shape=(sds(up_state, F32), sds(dn_state, F32)) * 3 + (sds((2, 1, SEQ, D), BF16),),
+        in_specs=[any_spec] * 7,
+        out_specs=(any_spec,) * 7,
+        scratch_shapes=[pltpu.VMEM(up_state, F32), pltpu.VMEM(dn_state, F32)] * 3 + [pltpu.VMEM((2, 1, SEQ, D), BF16)] + [
+            dma((7, 2)), dma((7, 2))],
+        compiler_params=pltpu.CompilerParams(vmem_limit_bytes=67043328),
+    )
+
     def device_step(*args):
-        return call(*args)
+        return emit(*call(*args))
 
     return jax.shard_map(device_step, mesh=mesh, in_specs=(layer_spec, tok_spec, tok_spec, rep_spec, rep_spec) + (layer_spec,) * 8,
                          out_specs=(layer_spec,) * 6 + (tok_spec,), check_vma=False)

time: 231 us -> 217 us (0.939)
  local copies, waits for them, and re-layouts: 10.7 us -> 0 us
  Pallas kernels: 219 us -> 216 us
    unnamed x17 -> x0, local copies, waits for them, and re-layouts: 10.7 us -> none
    pallas_call x1 -> x2, Pallas kernels: 219 us -> 216 us  [device_step(): return emit(*call(*args))]
where the time goes in v3:
time: 217 us
  Pallas kernels  216 us (100%)
    pallas_call x2, Pallas kernels, device_step(): return emit(*call(*args))  216 us

profile of v3, /device:TPU:0, one launch (start us, length us, event | category | flops | bytes accessed | tf_op | source)
XLA Modules:
  0.0 216.6 jit_solution(3874151888484888047)
XLA Ops:
  0.6 208.0 %shard_map.180 = (f32[2,2,32,2048]{3,2,1,0:T(8,128)}, f32[2,2,128,512]{3,2,1,0:T(8,128)}, f32[2,2,32,2048]{3,2,1,0:T(8,128)}, f32[2,2,128,512]{3,2,1,0:T(8,128)}...) custom-call(bf16[2,2,1,2048,512]{4,3,2,1,0:T(8,128)(2,1)} %x_saved.1, ...), custom_call_target="tpu_custom_call" | custom-call | tf_op jit(solution)/shard_map/pallas_call | solution.py:540
  208.6 7.9 %shard_map.181 = (f32[2,2,32,2048]{3,2,1,0:T(8,128)}, f32[2,2,128,512]{3,2,1,0:T(8,128)}, f32[2,2,32,2048]{3,2,1,0:T(8,128)}, f32[2,2,128,512]{3,2,1,0:T(8,128)}...) custom-call(f32[2,2,32,2048]{3,2,1,0:T(8,128)} %get-tuple-element.14.refs_0_, ...), custom_call_target="tpu_custom_call" | custom-call | tf_op jit(solution)/shard_map/pallas_call | solution.py:540

commit v4 on v3

--- a/solution.py
+++ b/solution.py
@@ -101,7 +101,7 @@
                 o_mas_up, o_mas_dn, o_mo_up, o_mo_dn, o_ve_up, o_ve_dn, y_out,
                 xs_top, xs_low, dyb, dxa, w1, w2, sent_up, sent_dn, recv_up, recv_dn,
                 s_acc_up, s_mas_up, s_mo_up, s_ve_up,
-                own_up, own_dn, acc1, acc2, act_buf, dh_buf,
+                own_up, own_dn, acc1, acc2,
                 load_sem, tok_send, tok_recv, rs_send, rs_recv, ag_send, ag_recv, out_sem, y_sem, free_sem):
     me = lax.axis_index('fsdp')
     stage = lax.rem(me, 2)
@@ -169,6 +169,12 @@
         c.start()
     for c in loads[4:]:
         c.start()
+
+    def zero_body(b, _):
+        dxa[b // 4, pl.ds(pl.multiple_of(lax.rem(b, 4) * 512, 512), 512), :] = jnp.zeros((512, D), F32)
+        return 0
+
+    lax.fori_loop(0, 8, zero_body, 0)
     for c in loads[:4]:
         c.wait()
 
@@ -193,47 +199,38 @@
     up_dests = [2 * chip_at(m) + core for m in ORDER[:-1] for core in range(2)] + [partner]
 
     def backward(layer, xs, with_dx, first_waits):
-        def chunk_body(t, _):
+        def chunk_body(t, _, peeled=False):
             chunk = chip_xor(pick(ORDER, t))
             cols = pl.ds(pl.multiple_of(chunk * FC, FC), FC)
 
-            def token_body(q, _):
-                @pl.when(jnp.logical_and(t == 0, q == 1))
-                def _():
+            def token_body(q):
+                if q == 1 and peeled:
                     for c in first_waits:
                         c.wait_recv()
 
-                @pl.when(q == 0)
-                def _():
-                    acc1[...] = jnp.zeros_like(acc1)
-                    acc2[...] = jnp.zeros_like(acc2)
-
                 x = xs[q]
                 dy = dyb[q]
+                tmp = sent_dn.at[0] if layer == 1 else xs_top.at[0]
                 for lo in range(0, SEQ, SUB):
                     part_rows = slice(lo, lo + SUB)
                     hidden = dot_nn(x[part_rows], w1[layer, :, cols])
                     grad_act = dot_nt(dy[part_rows], w2[layer, cols, :])
-                    act_buf[part_rows, :], dh_buf[part_rows, :] = gelu_and_grad(hidden, grad_act)
-                act = act_buf[...]
-                grad_hidden = dh_buf[...]
-                acc2[...] += dot_tn(act, dy)
-                acc1[...] += dot_tn(x, grad_hidden)
+                    tmp[part_rows, :FC], tmp[part_rows, FC:] = gelu_and_grad(hidden, grad_act)
+                act = tmp[:, :FC]
+                grad_hidden = tmp[:, FC:]
+                part_dn = dot_tn(act, dy)
+                part_up = dot_tn(x, grad_hidden)
+                if q == 0:
+                    acc2[...] = part_dn
+                    acc1[...] = part_up
+                else:
+                    sent_dn[layer, cols, :] = (acc2[...] + part_dn).astype(BF16)
+                    sent_up[layer, chunk] = (acc1[...] + part_up).astype(BF16)
                 if with_dx:
-                    part = dot_nt(grad_hidden, w1[layer, :, cols])
-
-                    @pl.when(t == 0)
-                    def _():
-                        dxa[q] = part
-
-                    @pl.when(t > 0)
-                    def _():
-                        dxa[q] += part
-                return 0
-
-            lax.fori_loop(0, 2, token_body, 0)
-            sent_up[layer, chunk] = acc1[...].astype(BF16)
-            sent_dn[layer, cols, :] = acc2[...].astype(BF16)
+                    dxa[q] += dot_nt(grad_hidden, w1[layer, :, cols])
+
+            token_body(0)
+            token_body(1)
 
             @pl.when(t < NCHUNK - 1)
             def _():
@@ -251,7 +248,12 @@
             recv_up[layer, chunk, own_rows, :] = sent_up[layer, chunk, own_rows, :]
             return 0
 
-        lax.fori_loop(0, NCHUNK, chunk_body, 0)
+        if with_dx:
+            chunk_body(0, 0, True)
+        else:
+            for c in first_waits:
+                c.wait_recv()
+        lax.fori_loop(1 if with_dx else 0, NCHUNK, chunk_body, 0)
 
     backward(1, xs_top, True, pushes[:2])
     pl.semaphore_signal(free_sem, inc=1, device_id=(partner,), device_id_type=MESH)
@@ -519,7 +521,6 @@
         ] + [pltpu.VMEM(up_state, F32)] * 4 + [
             pltpu.VMEM((2, 2, UP_ROWS, FF), BF16), pltpu.VMEM((2, 2, DOWN_ROWS, D), BF16),
             pltpu.VMEM((D, FC), F32), pltpu.VMEM((FC, D), F32),
-            pltpu.VMEM((SEQ, FC), BF16), pltpu.VMEM((SEQ, FC), BF16),
             dma((27,)), dma((4,)), dma((4,)), dma((2, 2)), dma((2, 2)), dma((2, 2)), dma((2, 2, 8)),
             dma((2, 3, 3)), dma((3,)), pltpu.SemaphoreType.REGULAR,
         ],

time: 217 us -> 208 us (0.959)
  Pallas kernels: 216 us -> 207 us
    pallas_call x2, Pallas kernels: 216 us -> 207 us  [device_step(): return emit(*call(*args))]
where the time goes in v4:
time: 208 us
  Pallas kernels  207 us (100%)
    pallas_call x2, Pallas kernels, device_step(): return emit(*call(*args))  207 us

profile of v4, /device:TPU:0, one launch (start us, length us, event | category | flops | bytes accessed | tf_op | source)
XLA Modules:
  0.0 207.8 jit_solution(8851149147728636297)
XLA Ops:
  0.6 199.1 %shard_map.180 = (f32[2,2,32,2048]{3,2,1,0:T(8,128)}, f32[2,2,128,512]{3,2,1,0:T(8,128)}, f32[2,2,32,2048]{3,2,1,0:T(8,128)}, f32[2,2,128,512]{3,2,1,0:T(8,128)}...) custom-call(bf16[2,2,1,2048,512]{4,3,2,1,0:T(8,128)(2,1)} %x_saved.1, ...), custom_call_target="tpu_custom_call" | custom-call | tf_op jit(solution)/shard_map/pallas_call | solution.py:541
  199.8 7.9 %shard_map.181 = (f32[2,2,32,2048]{3,2,1,0:T(8,128)}, f32[2,2,128,512]{3,2,1,0:T(8,128)}, f32[2,2,32,2048]{3,2,1,0:T(8,128)}, f32[2,2,128,512]{3,2,1,0:T(8,128)}...) custom-call(f32[2,2,32,2048]{3,2,1,0:T(8,128)} %get-tuple-element.14.refs_0_, ...), custom_call_target="tpu_custom_call" | custom-call | tf_op jit(solution)/shard_map/pallas_call | solution.py:541

commit v5 on v4

--- a/solution.py
+++ b/solution.py
@@ -170,11 +170,6 @@
     for c in loads[4:]:
         c.start()
 
-    def zero_body(b, _):
-        dxa[b // 4, pl.ds(pl.multiple_of(lax.rem(b, 4) * 512, 512), 512), :] = jnp.zeros((512, D), F32)
-        return 0
-
-    lax.fori_loop(0, 8, zero_body, 0)
     for c in loads[:4]:
         c.wait()
 
@@ -227,7 +222,8 @@
                     sent_dn[layer, cols, :] = (acc2[...] + part_dn).astype(BF16)
                     sent_up[layer, chunk] = (acc1[...] + part_up).astype(BF16)
                 if with_dx:
-                    dxa[q] += dot_nt(grad_hidden, w1[layer, :, cols])
+                    part_x = dot_nt(grad_hidden, w1[layer, :, cols])
+                    dxa[q] = part_x if peeled else dxa[q] + part_x
 
             token_body(0)
             token_body(1)
@@ -485,9 +481,13 @@
 def emit_kernel(*refs):
     src, dst, buf = refs[:7], refs[7:14], refs[14:21]
     in_sem, done_sem = refs[21:]
-    spots = [(i, half) for i in range(7) for half in range(2)]
-    into = [pltpu.make_async_copy(src[i].at[h], buf[i].at[h], in_sem.at[i, h]) for i, h in spots]
-    out = [pltpu.make_async_copy(buf[i].at[h], dst[i].at[h], done_sem.at[i, h]) for i, h in spots]
+    spots = [(i, h, j) for i in range(7) for h in range(2) for j in range(2)]
+
+    def piece(ref, i, h, j):
+        return ref.at[h, j] if i < 6 else ref.at[h, 0, pl.ds(j * (SEQ // 2), SEQ // 2), :]
+
+    into = [pltpu.make_async_copy(piece(src[i], i, h, j), piece(buf[i], i, h, j), in_sem.at[i, h, j]) for i, h, j in spots]
+    out = [pltpu.make_async_copy(piece(buf[i], i, h, j), piece(dst[i], i, h, j), done_sem.at[i, h, j]) for i, h, j in spots]
     for c in into:
         c.start()
     for c, d in zip(into, out):
@@ -533,7 +533,7 @@
         in_specs=[any_spec] * 7,
         out_specs=(any_spec,) * 7,
         scratch_shapes=[pltpu.VMEM(up_state, F32), pltpu.VMEM(dn_state, F32)] * 3 + [pltpu.VMEM((2, 1, SEQ, D), BF16)] + [
-            dma((7, 2)), dma((7, 2))],
+            dma((7, 2, 2)), dma((7, 2, 2))],
         compiler_params=pltpu.CompilerParams(vmem_limit_bytes=67043328),
     )
 

time: 208 us -> 208 us (level)
  no operation moved by 1% of the time
where the time goes in v5:
time: 208 us; the launch traced here: 207 us
  Pallas kernels  207 us (100%)
    pallas_call x2, Pallas kernels, device_step(): return emit(*call(*args))  207 us

profile of v5, /device:TPU:0, one launch (start us, length us, event | category | flops | bytes accessed | tf_op | source)
XLA Modules:
  0.0 207.4 jit_solution(16688055995175539594)
XLA Ops:
  0.6 198.6 %shard_map.180 = (f32[2,2,32,2048]{3,2,1,0:T(8,128)}, f32[2,2,128,512]{3,2,1,0:T(8,128)}, f32[2,2,32,2048]{3,2,1,0:T(8,128)}, f32[2,2,128,512]{3,2,1,0:T(8,128)}...) custom-call(bf16[2,2,1,2048,512]{4,3,2,1,0:T(8,128)(2,1)} %x_saved.1, ...), custom_call_target="tpu_custom_call" | custom-call | tf_op jit(solution)/shard_map/pallas_call | solution.py:541
  199.2 8.0 %shard_map.181 = (f32[2,2,32,2048]{3,2,1,0:T(8,128)}, f32[2,2,128,512]{3,2,1,0:T(8,128)}, f32[2,2,32,2048]{3,2,1,0:T(8,128)}, f32[2,2,128,512]{3,2,1,0:T(8,128)}...) custom-call(f32[2,2,32,2048]{3,2,1,0:T(8,128)} %get-tuple-element.14.refs_0_, ...), custom_call_target="tpu_custom_call" | custom-call | tf_op jit(solution)/shard_map/pallas_call | solution.py:541
